TPU v7x, 512 devices: a whole 4x8x8 slice. The times are simulated.
512 devices in a mesh: vocab: 64 (over z, y), pipe: 8 (over x, core).
Axes of the slice: x: 4, y: 8, z: 8, core: 2. Of those that a mesh axis runs over, the one named last changes fastest.
Arguments:
- hidden_a: bfloat16 [2048, 4096], P('pipe', 'vocab'), parts along dimension 0, may hold values from -8 to 8, as said below
- labels_a: int32 [2048], P('pipe'), parts along dimension 0, may hold values from 0 to 32767
- hidden_b: bfloat16 [2048, 4096], P('pipe', 'vocab'), parts along dimension 0, may hold values from -8 to 8, as said below
- labels_b: int32 [2048], P('pipe'), parts along dimension 0, may hold values from 0 to 32767
- loss_cotangent: float32 [2048], P('pipe'), parts along dimension 0, may hold values from -192 to 192
- out_weight: bfloat16 [32768, 32768], P('pipe', 'vocab'), parts along dimension 0, may hold values from -0.28125 to 0.28125, as said below
Outputs:
- logits_a: bfloat16 [2048, 32768], P('pipe', 'vocab'), parts along dimension 0
- loss_a: float32 [2048], P('pipe'), parts along dimension 0
- amax_scale: float32 [8], P('pipe'), parts along dimension 0
- grad_hidden_b: bfloat16 [2048, 4096], P('pipe', 'vocab'), parts along dimension 0
There are 8 independent parts, one for each index of `pipe`. A program takes and returns all parts, laid end to end along the dimension named above; each array names one. Nothing has to cross between parts.
Inputs may be any that keep to these rules, and one draw needn't show every extreme that they name: `hidden_a`: hidden states of order one. `hidden_b`: hidden states of order one. `out_weight`: entries of scale 3 over the square root of 4096.
All inputs are finite; a program needn't handle non-finite values. Where the computation divides by a largest or mean magnitude, that divisor is 1e-20 or more.
Results may differ from a plain program's by a relative error of at most 0.0048.
Values may be sent and summed in bfloat16 or wider, within the bound.
No kernel may reach another device: no remote copies, remote signals or barrier semaphores. Data moves between devices by JAX's collectives and lax.ppermute only.
A program may use at most 64 MiB of HBM per device.

v0:
```python
import jax
import jax.numpy as jnp
from jax import lax
from jax.sharding import Mesh
from jax.sharding import PartitionSpec as P


Z, Y = ("z_two", "z_one"), ("y_two", "y_one")
VOCAB = (*Z, *Y)
LATTICE = ("z_two", "y_two")
FLIPS = ((1, 0), (0, 1), (1, 1))


def size(axes):
    return lax.axis_size(axes)


def from_everyone(x, axes):
    return lax.all_to_all(jnp.broadcast_to(x[None], (size(axes), *x.shape)), axes, 0, 0, tiled=True)


def neighbour(i, n, shift):
    return (i + 1 - 2 * ((i + shift) % 2) + n) % n


def exchanged(x, flip, shift):
    nz, ny = size(Z), size(Y)
    pairs = []
    for z in range(nz):
        for y in range(ny):
            there = neighbour(z, nz, shift) if flip[0] else z, neighbour(y, ny, shift) if flip[1] else y
            pairs.append((z * ny + y, there[0] * ny + there[1]))
    return lax.ppermute(x, VOCAB, pairs)


def shards(hidden_a, labels_a, hidden_b, labels_b, loss_cotangent, out_weight):
    tokens, width = hidden_a.shape
    columns = out_weight.shape[1]
    offset = lax.axis_index(VOCAB) * columns
    lattice = size(LATTICE)
    half = lattice * width // 2
    by_class = out_weight.reshape(size(Z[0]), 2, size(Y[0]), 2, width, columns)

    def weight_rows(flip):
        z, y = lax.axis_index(Z[1]), lax.axis_index(Y[1])
        at = (0, z + flip[0] - 2 * z * flip[0], 0, y + flip[1] - 2 * y * flip[1], 0, 0)
        counts = (by_class.shape[0], 1, by_class.shape[2], 1, width, columns)
        return lax.dynamic_slice(by_class, at, counts).reshape(2 * half, columns)

    weights = {flip: weight_rows(flip) for flip in ((0, 0), *FLIPS)}

    def product(block, rows):
        return lax.dot_general(
            block, rows, (((0,), (0,)), ((), ())), preferred_element_type=jnp.float32
        )

    def class_rows(hidden):
        return from_everyone(hidden.T, LATTICE).reshape(2 * half, tokens)

    mine_b = class_rows(hidden_b)
    mine_a = class_rows(hidden_a)
    scores_b = product(mine_b, weights[0, 0])
    for flip in FLIPS:
        for shift in range(2):
            at = slice(shift * half, (shift + 1) * half)
            block = exchanged(mine_b[at], flip, shift)
            scores_b = scores_b + product(block, weights[flip][at])
    scores_a = product(mine_a, weights[0, 0])
    for flip in FLIPS:
        block = exchanged(mine_a, flip, 1)
        scores_a = scores_a + product(block, weights[flip])
    column = offset + lax.broadcasted_iota(jnp.int32, (1, columns), 1)
    column_a = lax.optimization_barrier(column)

    def log_total(scores):
        peak = jnp.max(scores, axis=1)
        return peak + jnp.log(jnp.sum(jnp.exp(scores - peak[:, None]), axis=1))

    def joined(logs):
        peak = jnp.max(logs, axis=0)
        return peak + jnp.log(jnp.sum(jnp.exp(logs - peak), axis=0))

    log_b = joined(from_everyone(log_total(scores_b).reshape(1, -1), VOCAB).reshape(-1, tokens))
    label_own = jnp.sum(jnp.where(column_a == labels_a[:, None], scores_a, 0.0), axis=1)
    largest = jnp.full((128,), jnp.max(jnp.abs(scores_a)))
    line = jnp.concatenate([log_total(scores_a), label_own, largest])
    lines = from_everyone(line.reshape(1, -1), VOCAB).reshape(-1, line.size)
    loss_a = joined(lines[:, :tokens]) - jnp.sum(lines[:, tokens : 2 * tokens], axis=0)
    amax_scale = (448.0 / jnp.max(lines[:, 2 * tokens :])).reshape(1).astype(jnp.float32)

    onehot = (column == labels_b[:, None]).astype(jnp.float32)
    dlogits_b = ((jnp.exp(scores_b - log_b[:, None]) - onehot) * loss_cotangent[:, None]).astype(
        jnp.bfloat16
    )

    dlogits_b = lax.optimization_barrier(dlogits_b)

    def grad_rows(flip):
        return lax.dot_general(
            weights[flip], dlogits_b, (((1,), (1,)), ((), ())), preferred_element_type=jnp.float32
        )

    total = grad_rows((0, 0))
    for flip in FLIPS:
        total = total + exchanged(grad_rows(flip).astype(jnp.bfloat16), flip, 0).astype(jnp.float32)
    parts = total.astype(jnp.bfloat16).reshape(lattice, width, tokens)
    parts = lax.all_to_all(parts, LATTICE, 0, 0, tiled=True)
    grad_hidden_b = jnp.sum(parts.astype(jnp.float32), axis=0).astype(jnp.bfloat16).T
    return (scores_a.astype(jnp.bfloat16), loss_a, amax_scale, grad_hidden_b)


def solution(mesh):
    finer = Mesh(mesh.devices.reshape(4, 2, 4, 2, mesh.shape["pipe"]), (*VOCAB, "pipe"))
    placed = (P("pipe", VOCAB), P("pipe"), P("pipe", VOCAB), P("pipe"), P("pipe"), P("pipe", VOCAB))

    return jax.shard_map(
        shards,
        mesh=finer,
        in_specs=placed,
        out_specs=(P("pipe", VOCAB), P("pipe"), P("pipe"), P("pipe", VOCAB)),
        check_vma=False,
    )
```

profile of v0, /device:TPU:2, one launch (start us, length us, event | category | flops | bytes accessed | tf_op | source)
XLA Modules:
  0.0 177.7 jit_solution(9862571332019461231)
XLA Ops:
  0.6 1.6 broadcast_in_dim.18
  2.2 15.7 %all-to-all-start.2 = ((bf16[16,64,256]{2,1,0:T(8,128)(2,1)}), bf16[16,64,256]{2,1,0:T(8,128)(2,1)}, u32[]{:S(2)}, u32[]{:S(2)}) async-start(bf16[16,64,256]{2,1,0:T(8,128)(2,1)} %broadcast_in_dim.18), calls=%async_computation.2 | async-start | bytes 1048576 | tf_op jit(solution)/shard_map/all_to_all | solution.py:19
  18.0 0.0 copy-start
  18.0 3.7 %constant_dynamic-slice_fusion.4 = (bf16[2,1,4,1,64,512]{5,4,3,2,1,0:T(8,128)(2,1)}, bf16[2,1,4,1,64,512]{5,4,3,2,1,0:T(8,128)(2,1)}, bf16[2,1,4,1,64,512]{5,4,3...) fusion(bf16[4,2,4,2,64,512]{5,4,3,2,1,0:T(8,128)(2,1)} %bitcast, ...), kind=kLoop, calls=%fused_computation.38 | loop fusion | bytes 6291476 | tf_op jit(solution)/shard_map/slice | solution.py:67
  21.7 1.4 constant_dynamic-slice_fusion.7
  23.1 14.8 %all-to-all-done.2 = bf16[16,64,256]{2,1,0:T(8,128)(2,1)} async-done(((bf16[16,64,256]{2,1,0:T(8,128)(2,1)}), bf16[16,64,256]{2,1,0:T(8,128)(2,1)}, u32[]{:S(2)}, u32[]{:S(2)}) %all-to-all-start.2) | async-done | bytes 524320 | tf_op jit(solution)/shard_map/all_to_all | solution.py:19
  38.0 0.9 broadcast_in_dim.13
  38.8 6.2 %all-to-all-start = ((bf16[16,64,256]{2,1,0:T(8,128)(2,1)}), bf16[16,64,256]{2,1,0:T(8,128)(2,1)}, u32[]{:S(2)}, u32[]{:S(2)}) async-start(bf16[16,64,256]{2,1,0:T(8,128)(2,1)} %broadcast_in_dim.13), calls=%async_computation | async-start | bytes 1048576 | tf_op jit(solution)/shard_map/all_to_all | solution.py:19
  45.1 1.2 fusion.13
  46.3 3.4 %collective-permute-start.3 = (bf16[512,256]{1,0:T(8,128)(2,1)S(1)}, bf16[512,256]{1,0:T(8,128)(2,1)S(1)}, u32[]{:S(2)}, u32[]{:S(2)}) collective-permute-start(bf16[512,256]{1,0:T(8,128)(2,1)S(1)} %bitcast.102), channel_id=1, source_target_pairs={{0,64},{8,72},{16,80},{24,88},{32,96},{40,104},{48,112},{56,120},{... | collective-permute-start | bytes 786440 | tf_op jit(solution)/shard_map/ppermute | solution.py:33
  49.7 1.9 %collective-permute-start.5 = (bf16[512,256]{1,0:T(8,128)(2,1)S(1)}, bf16[512,256]{1,0:T(8,128)(2,1)S(1)}, u32[]{:S(2)}, u32[]{:S(2)}) collective-permute-start(bf16[512,256]{1,0:T(8,128)(2,1)S(1)} %bitcast.103), channel_id=1, source_target_pairs={{0,8},{8,0},{16,24},{24,16},{32,40},{40,32},{48,56},{56,48},{64,72... | collective-permute-start | bytes 786440 | tf_op jit(solution)/shard_map/ppermute | solution.py:33
  51.6 4.0 %collective-permute-start.7 = (bf16[512,256]{1,0:T(8,128)(2,1)S(1)}, bf16[512,256]{1,0:T(8,128)(2,1)S(1)}, u32[]{:S(2)}, u32[]{:S(2)}) collective-permute-start(bf16[512,256]{1,0:T(8,128)(2,1)S(1)} %bitcast.104), channel_id=1, source_target_pairs={{0,72},{8,64},{16,88},{24,80},{32,104},{40,96},{48,120},{56,112},{... | collective-permute-start | bytes 786440 | tf_op jit(solution)/shard_map/ppermute | solution.py:33
  55.6 4.4 %collective-permute-start.6 = (bf16[512,256]{1,0:T(8,128)(2,1)S(1)}, bf16[512,256]{1,0:T(8,128)(2,1)S(1)}, u32[]{:S(2)}, u32[]{:S(2)}) collective-permute-start(bf16[512,256]{1,0:T(8,128)(2,1)S(1)} %bitcast.99), channel_id=1, source_target_pairs={{0,56},{8,16},{16,8},{24,32},{32,24},{40,48},{48,40},{56,0},{64,12... | collective-permute-start | bytes 786440 | tf_op jit(solution)/shard_map/ppermute | solution.py:33
  60.1 5.9 %collective-permute-start.8 = (bf16[512,256]{1,0:T(8,128)(2,1)S(1)}, bf16[512,256]{1,0:T(8,128)(2,1)S(1)}, u32[]{:S(2)}, u32[]{:S(2)}) collective-permute-start(bf16[512,256]{1,0:T(8,128)(2,1)S(1)} %bitcast.100), channel_id=1, source_target_pairs={{0,504},{8,464},{16,456},{24,480},{32,472},{40,496},{48,488},{56,4... | collective-permute-start | bytes 786440 | tf_op jit(solution)/shard_map/ppermute | solution.py:33
  66.0 1.6 fusion.18
  67.6 2.3 %collective-permute-done.3 = bf16[512,256]{1,0:T(8,128)(2,1)S(1)} collective-permute-done((bf16[512,256]{1,0:T(8,128)(2,1)S(1)}, bf16[512,256]{1,0:T(8,128)(2,1)S(1)}, u32[]{:S(2)}, u32[]{:S(2)}) %collective-permute-start.3) | collective-permute-done | bytes 262176 | tf_op jit(solution)/shard_map/ppermute | solution.py:33
  69.9 5.7 %collective-permute-start.4 = (bf16[512,256]{1,0:T(8,128)(2,1)S(1)}, bf16[512,256]{1,0:T(8,128)(2,1)S(1)}, u32[]{:S(2)}, u32[]{:S(2)}) collective-permute-start(bf16[512,256]{1,0:T(8,128)(2,1)S(1)} %bitcast.101), channel_id=1, source_target_pairs={{0,448},{8,456},{16,464},{24,472},{32,480},{40,488},{48,496},{56,5... | collective-permute-start | bytes 786440 | tf_op jit(solution)/shard_map/ppermute | solution.py:33
  75.6 1.4 convolution_add_fusion.3
  77.0 0.0 collective-permute-done.5
  77.0 0.3 fusion.19
  77.4 0.0 collective-permute-done.6
  77.4 0.3 fusion.20
  77.8 0.3 fusion.21
  78.1 0.0 collective-permute-done.8
  78.1 0.0 copy-start.11
  78.2 0.0 copy-start.12
  78.2 0.3 fusion.22
  78.5 2.6 %collective-permute-done.4 = bf16[512,256]{1,0:T(8,128)(2,1)S(1)} collective-permute-done((bf16[512,256]{1,0:T(8,128)(2,1)S(1)}, bf16[512,256]{1,0:T(8,128)(2,1)S(1)}, u32[]{:S(2)}, u32[]{:S(2)}) %collective-permute-start.4) | collective-permute-done | bytes 262176 | tf_op jit(solution)/shard_map/ppermute | solution.py:33
  81.1 0.4 fusion.15
  81.5 0.1 exponential_reduce_fusion
  81.6 0.7 broadcast_in_dim.19
  82.3 10.1 %all-to-all-start.3 = ((f32[64,1,256]{2,1,0:T(1,128)}), f32[64,1,256]{2,1,0:T(1,128)S(1)}, u32[]{:S(2)}, u32[]{:S(2)}) async-start(f32[64,1,256]{2,1,0:T(1,128)} %broadcast_in_dim.19), calls=%async_computation.3 | async-start | bytes 131072 | tf_op jit(solution)/shard_map/all_to_all | solution.py:19
  92.4 2.6 %fusion.16 = f32[512,256]{1,0:T(8,128)} fusion(bf16[1024,512]{1,0:T(8,128)(2,1)} %bitcast.88, bf16[1024,256]{1,0:T(8,128)(2,1)} %bitcast.3), kind=kOutput, calls=%fused_computation.53 | convolution fusion | flops 268435456 | bytes 2097152 | tf_op jit(solution)/shard_map/dot_general | solution.py:53
  95.0 4.9 %collective-permute-start = (bf16[1024,256]{1,0:T(8,128)(2,1)}, bf16[1024,256]{1,0:T(8,128)(2,1)}, u32[]{:S(2)}, u32[]{:S(2)}) collective-permute-start(bf16[1024,256]{1,0:T(8,128)(2,1)} %bitcast.3), channel_id=1, source_target_pairs={{0,448},{8,456},{16,464},{24,472},{32,480},{40,488},{48,496},{56,5... | collective-permute-start | bytes 1572872 | tf_op jit(solution)/shard_map/ppermute | solution.py:33
  100.0 4.3 %collective-permute-start.2 = (bf16[1024,256]{1,0:T(8,128)(2,1)}, bf16[1024,256]{1,0:T(8,128)(2,1)}, u32[]{:S(2)}, u32[]{:S(2)}) collective-permute-start(bf16[1024,256]{1,0:T(8,128)(2,1)} %bitcast.3), channel_id=1, source_target_pairs={{0,504},{8,464},{16,456},{24,480},{32,472},{40,496},{48,488},{56,4... | collective-permute-start | bytes 1572872 | tf_op jit(solution)/shard_map/ppermute | solution.py:33
  104.3 2.4 %collective-permute-start.1 = (bf16[1024,256]{1,0:T(8,128)(2,1)}, bf16[1024,256]{1,0:T(8,128)(2,1)}, u32[]{:S(2)}, u32[]{:S(2)}) collective-permute-start(bf16[1024,256]{1,0:T(8,128)(2,1)} %bitcast.3), channel_id=1, source_target_pairs={{0,56},{8,16},{16,8},{24,32},{32,24},{40,48},{48,40},{56,0},{64,12... | collective-permute-start | bytes 1572872 | tf_op jit(solution)/shard_map/ppermute | solution.py:33
  106.7 0.0 all-to-all-done.3
  106.7 0.1 reduce_max.59
  106.8 0.2 fusion.6
  107.0 1.2 convolution_convert_fusion.2
  108.3 2.3 %collective-permute-start.9 = (bf16[1024,256]{1,0:T(8,128)(2,1)}, bf16[1024,256]{1,0:T(8,128)(2,1)}, u32[]{:S(2)}, u32[]{:S(2)}) collective-permute-start(bf16[1024,256]{1,0:T(8,128)(2,1)} %convolution_convert_fusion.2), channel_id=1, source_target_pairs={{0,64},{8,72},{16,80},{24,88},{32,96},{40,104},{48,112},{56,120},{... | collective-permute-start | bytes 1572872 | tf_op jit(solution)/shard_map/ppermute | solution.py:33
  110.5 1.2 convolution_convert_fusion.1
  111.8 2.2 %collective-permute-start.10 = (bf16[1024,256]{1,0:T(8,128)(2,1)}, bf16[1024,256]{1,0:T(8,128)(2,1)}, u32[]{:S(2)}, u32[]{:S(2)}) collective-permute-start(bf16[1024,256]{1,0:T(8,128)(2,1)} %convolution_convert_fusion.1), channel_id=1, source_target_pairs={{0,8},{8,0},{16,24},{24,16},{32,40},{40,32},{48,56},{56,48},{64,72... | collective-permute-start | bytes 1572872 | tf_op jit(solution)/shard_map/ppermute | solution.py:33
  113.9 1.2 convolution_convert_fusion
  115.2 5.1 %collective-permute-done.2 = bf16[1024,256]{1,0:T(8,128)(2,1)} collective-permute-done((bf16[1024,256]{1,0:T(8,128)(2,1)}, bf16[1024,256]{1,0:T(8,128)(2,1)}, u32[]{:S(2)}, u32[]{:S(2)}) %collective-permute-start.2) | collective-permute-done | bytes 524320 | tf_op jit(solution)/shard_map/ppermute | solution.py:33
  120.3 1.9 %collective-permute-start.11 = (bf16[1024,256]{1,0:T(8,128)(2,1)}, bf16[1024,256]{1,0:T(8,128)(2,1)}, u32[]{:S(2)}, u32[]{:S(2)}) collective-permute-start(bf16[1024,256]{1,0:T(8,128)(2,1)} %convolution_convert_fusion), channel_id=1, source_target_pairs={{0,72},{8,64},{16,88},{24,80},{32,104},{40,96},{48,120},{56,112},{... | collective-permute-start | bytes 1572872 | tf_op jit(solution)/shard_map/ppermute | solution.py:33
  122.2 1.5 fusion.17
  123.7 1.5 convolution_add_fusion.1
  125.3 1.5 collective-permute-done.1
  126.8 1.5 fusion.14
  128.4 0.7 fusion.8
  129.0 0.7 broadcast_in_dim.16
  129.7 0.8 broadcast_in_dim.17
  130.5 12.4 %all-to-all-start.1 = ((f32[64,1,640]{2,1,0:T(1,128)}), f32[64,1,640]{2,1,0:T(1,128)S(1)}, u32[]{:S(2)}, u32[]{:S(2)}) async-start(f32[64,1,640]{2,1,0:T(1,128)} %broadcast_in_dim.17), calls=%async_computation.1 | async-start | bytes 327680 | tf_op jit(solution)/shard_map/all_to_all | solution.py:19
  142.9 0.0 collective-permute-done.10
  142.9 0.0 collective-permute-done.11
  142.9 2.6 %add_convert_fusion = bf16[1024,256]{1,0:T(8,128)(2,1)} fusion(bf16[1024,256]{1,0:T(8,128)(2,1)} %collective-permute-done.11, bf16[1024,256]{1,0:T(8,128)(2,1)} %collective-permute-done.10, bf16[1024,256]{1,0:T(8,128)(2,1)} %collective-permute-done.9, bf16[1024,512]{1,0:T(8,128)(2,1)S(1)} %bitcast.89, bf16[256,512]{0,1:T(8,128)(2,1)S(1)} %fusion.6), kind=kOutput, calls=%fused_computation.12 | convolution fusion | flops 270270464 | bytes 3407872 | tf_op jit(solution)/shard_map/dot_general | solution.py:99
  145.5 10.3 %all-to-all-done.1 = f32[64,1,640]{2,1,0:T(1,128)S(1)} async-done(((f32[64,1,640]{2,1,0:T(1,128)}), f32[64,1,640]{2,1,0:T(1,128)S(1)}, u32[]{:S(2)}, u32[]{:S(2)}) %all-to-all-start.1) | async-done | bytes 163872 | tf_op jit(solution)/shard_map/all_to_all | solution.py:19
  155.8 3.6 %all-to-all-start.4 = ((bf16[16,64,256]{2,1,0:T(8,128)(2,1)}), bf16[16,64,256]{2,1,0:T(8,128)(2,1)S(1)}, u32[]{:S(2)}, u32[]{:S(2)}) async-start(bf16[16,64,256]{2,1,0:T(8,128)(2,1)} %bitcast.21), calls=%async_computation.4 | async-start | bytes 1048576 | tf_op jit(solution)/shard_map/all_to_all | solution.py:107
  159.4 0.8 copy.13
  160.2 0.6 slice_reduce_fusion.2
  161.6 0.6 add_subtract_fusion
  162.2 13.7 %all-to-all-done.4 = bf16[16,64,256]{2,1,0:T(8,128)(2,1)S(1)} async-done(((bf16[16,64,256]{2,1,0:T(8,128)(2,1)}), bf16[16,64,256]{2,1,0:T(8,128)(2,1)S(1)}, u32[]{:S(2)}, u32[]{:S(2)}) %all-to-all-start.4) | async-done | bytes 524320 | tf_op jit(solution)/shard_map/all_to_all | solution.py:107
  175.8 0.7 reduce_sum.72
  (39 shorter events, 0.2 us)
Async XLA Ops:
  2.2 35.7 %all-to-all-start.2 = ((bf16[16,64,256]{2,1,0:T(8,128)(2,1)}), bf16[16,64,256]{2,1,0:T(8,128)(2,1)}, u32[]{:S(2)}, u32[]{:S(2)}) async-start(bf16[16,64,256]{2,1,0:T(8,128)(2,1)} %broadcast_in_dim.18), calls=%async_computation.2 | async-start | bytes 1048576 | tf_op jit(solution)/shard_map/all_to_all | solution.py:19
  18.0 3.7 %copy-start = (bf16[4096,512]{1,0:T(8,128)(2,1)S(1)}, bf16[4096,512]{1,0:T(8,128)(2,1)}, u32[]{:S(2)}) copy-start(bf16[4096,512]{1,0:T(8,128)(2,1)} %param.11) | copy-start | bytes 12582916
  21.7 16.2 %copy-start.10 = (bf16[256,64]{0,1:T(8,128)(2,1)S(1)}, bf16[256,64]{0,1:T(8,128)(2,1)}, u32[]{:S(2)}) copy-start(bf16[256,64]{0,1:T(8,128)(2,1)} %param.6) | copy-start | bytes 98308
  23.1 54.6 %copy-start.2 = (bf16[4,1,4,1,64,512]{5,4,3,2,1,0:T(8,128)(2,1)}, bf16[4,1,4,1,64,512]{5,4,3,2,1,0:T(8,128)(2,1)S(1)}, u32[]{:S(2)}) copy-start(bf16[4,1,4,1,64,512]{5,4,3,2,1,0:T(8,128)(2,1)S(1)} %get-tuple-element.30) | copy-start | bytes 3145732
  38.8 42.8 %all-to-all-start = ((bf16[16,64,256]{2,1,0:T(8,128)(2,1)}), bf16[16,64,256]{2,1,0:T(8,128)(2,1)}, u32[]{:S(2)}, u32[]{:S(2)}) async-start(bf16[16,64,256]{2,1,0:T(8,128)(2,1)} %broadcast_in_dim.13), calls=%async_computation | async-start | bytes 1048576 | tf_op jit(solution)/shard_map/all_to_all | solution.py:19
  45.0 32.0 %copy-start.8 = (bf16[2,1,4,1,64,512]{5,4,3,2,1,0:T(8,128)(2,1)S(1)}, bf16[2,1,4,1,64,512]{5,4,3,2,1,0:T(8,128)(2,1)}, u32[]{:S(2)}) copy-start(bf16[2,1,4,1,64,512]{5,4,3,2,1,0:T(8,128)(2,1)} %get-tuple-element.25) | copy-start | bytes 1572868
  45.1 32.3 %copy-start.7 = (bf16[2,1,4,1,64,512]{5,4,3,2,1,0:T(8,128)(2,1)S(1)}, bf16[2,1,4,1,64,512]{5,4,3,2,1,0:T(8,128)(2,1)}, u32[]{:S(2)}) copy-start(bf16[2,1,4,1,64,512]{5,4,3,2,1,0:T(8,128)(2,1)} %get-tuple-element.24) | copy-start | bytes 1572868
  45.1 32.7 %copy-start.6 = (bf16[2,1,4,1,64,512]{5,4,3,2,1,0:T(8,128)(2,1)S(1)}, bf16[2,1,4,1,64,512]{5,4,3,2,1,0:T(8,128)(2,1)}, u32[]{:S(2)}) copy-start(bf16[2,1,4,1,64,512]{5,4,3,2,1,0:T(8,128)(2,1)} %get-tuple-element.23) | copy-start | bytes 1572868
  46.3 31.9 %copy-start.5 = (bf16[2,1,4,1,64,512]{5,4,3,2,1,0:T(8,128)(2,1)S(1)}, bf16[2,1,4,1,64,512]{5,4,3,2,1,0:T(8,128)(2,1)}, u32[]{:S(2)}) copy-start(bf16[2,1,4,1,64,512]{5,4,3,2,1,0:T(8,128)(2,1)} %get-tuple-element.22) | copy-start | bytes 1572868
  46.3 23.6 %collective-permute-start.3 = (bf16[512,256]{1,0:T(8,128)(2,1)S(1)}, bf16[512,256]{1,0:T(8,128)(2,1)S(1)}, u32[]{:S(2)}, u32[]{:S(2)}) collective-permute-start(bf16[512,256]{1,0:T(8,128)(2,1)S(1)} %bitcast.102), channel_id=1, source_target_pairs={{0,64},{8,72},{16,80},{24,88},{32,96},{40,104},{48,112},{56,120},{... | collective-permute-start | bytes 786440 | tf_op jit(solution)/shard_map/ppermute | solution.py:33
  49.7 27.3 %collective-permute-start.5 = (bf16[512,256]{1,0:T(8,128)(2,1)S(1)}, bf16[512,256]{1,0:T(8,128)(2,1)S(1)}, u32[]{:S(2)}, u32[]{:S(2)}) collective-permute-start(bf16[512,256]{1,0:T(8,128)(2,1)S(1)} %bitcast.103), channel_id=1, source_target_pairs={{0,8},{8,0},{16,24},{24,16},{32,40},{40,32},{48,56},{56,48},{64,72... | collective-permute-start | bytes 786440 | tf_op jit(solution)/shard_map/ppermute | solution.py:33
  51.6 26.2 %collective-permute-start.7 = (bf16[512,256]{1,0:T(8,128)(2,1)S(1)}, bf16[512,256]{1,0:T(8,128)(2,1)S(1)}, u32[]{:S(2)}, u32[]{:S(2)}) collective-permute-start(bf16[512,256]{1,0:T(8,128)(2,1)S(1)} %bitcast.104), channel_id=1, source_target_pairs={{0,72},{8,64},{16,88},{24,80},{32,104},{40,96},{48,120},{56,112},{... | collective-permute-start | bytes 786440 | tf_op jit(solution)/shard_map/ppermute | solution.py:33
  55.6 21.7 %collective-permute-start.6 = (bf16[512,256]{1,0:T(8,128)(2,1)S(1)}, bf16[512,256]{1,0:T(8,128)(2,1)S(1)}, u32[]{:S(2)}, u32[]{:S(2)}) collective-permute-start(bf16[512,256]{1,0:T(8,128)(2,1)S(1)} %bitcast.99), channel_id=1, source_target_pairs={{0,56},{8,16},{16,8},{24,32},{32,24},{40,48},{48,40},{56,0},{64,12... | collective-permute-start | bytes 786440 | tf_op jit(solution)/shard_map/ppermute | solution.py:33
  60.1 18.0 %collective-permute-start.8 = (bf16[512,256]{1,0:T(8,128)(2,1)S(1)}, bf16[512,256]{1,0:T(8,128)(2,1)S(1)}, u32[]{:S(2)}, u32[]{:S(2)}) collective-permute-start(bf16[512,256]{1,0:T(8,128)(2,1)S(1)} %bitcast.100), channel_id=1, source_target_pairs={{0,504},{8,464},{16,456},{24,480},{32,472},{40,496},{48,488},{56,4... | collective-permute-start | bytes 786440 | tf_op jit(solution)/shard_map/ppermute | solution.py:33
  66.0 15.1 %copy-start.4 = (bf16[2,1,4,1,64,512]{5,4,3,2,1,0:T(8,128)(2,1)S(1)}, bf16[2,1,4,1,64,512]{5,4,3,2,1,0:T(8,128)(2,1)}, u32[]{:S(2)}) copy-start(bf16[2,1,4,1,64,512]{5,4,3,2,1,0:T(8,128)(2,1)} %get-tuple-element.21) | copy-start | bytes 1572868
  69.9 11.2 %collective-permute-start.4 = (bf16[512,256]{1,0:T(8,128)(2,1)S(1)}, bf16[512,256]{1,0:T(8,128)(2,1)S(1)}, u32[]{:S(2)}, u32[]{:S(2)}) collective-permute-start(bf16[512,256]{1,0:T(8,128)(2,1)S(1)} %bitcast.101), channel_id=1, source_target_pairs={{0,448},{8,456},{16,464},{24,472},{32,480},{40,488},{48,496},{56,5... | collective-permute-start | bytes 786440 | tf_op jit(solution)/shard_map/ppermute | solution.py:33
  78.1 28.7 %copy-start.11 = (f32[256]{0:T(256)S(1)}, f32[256]{0:T(256)}, u32[]{:S(2)}) copy-start(f32[256]{0:T(256)} %param.10) | copy-start | bytes 3076
  78.2 28.7 %copy-start.12 = (s32[256]{0:T(256)S(1)}, s32[256]{0:T(256)}, u32[]{:S(2)}) copy-start(s32[256]{0:T(256)} %param.9) | copy-start | bytes 3076
  82.3 24.4 %all-to-all-start.3 = ((f32[64,1,256]{2,1,0:T(1,128)}), f32[64,1,256]{2,1,0:T(1,128)S(1)}, u32[]{:S(2)}, u32[]{:S(2)}) async-start(f32[64,1,256]{2,1,0:T(1,128)} %broadcast_in_dim.19), calls=%async_computation.3 | async-start | bytes 131072 | tf_op jit(solution)/shard_map/all_to_all | solution.py:19
  95.0 28.7 %collective-permute-start = (bf16[1024,256]{1,0:T(8,128)(2,1)}, bf16[1024,256]{1,0:T(8,128)(2,1)}, u32[]{:S(2)}, u32[]{:S(2)}) collective-permute-start(bf16[1024,256]{1,0:T(8,128)(2,1)} %bitcast.3), channel_id=1, source_target_pairs={{0,448},{8,456},{16,464},{24,472},{32,480},{40,488},{48,496},{56,5... | collective-permute-start | bytes 1572872 | tf_op jit(solution)/shard_map/ppermute | solution.py:33
  100.0 20.3 %collective-permute-start.2 = (bf16[1024,256]{1,0:T(8,128)(2,1)}, bf16[1024,256]{1,0:T(8,128)(2,1)}, u32[]{:S(2)}, u32[]{:S(2)}) collective-permute-start(bf16[1024,256]{1,0:T(8,128)(2,1)} %bitcast.3), channel_id=1, source_target_pairs={{0,504},{8,464},{16,456},{24,480},{32,472},{40,496},{48,488},{56,4... | collective-permute-start | bytes 1572872 | tf_op jit(solution)/shard_map/ppermute | solution.py:33
  104.3 22.5 %collective-permute-start.1 = (bf16[1024,256]{1,0:T(8,128)(2,1)}, bf16[1024,256]{1,0:T(8,128)(2,1)}, u32[]{:S(2)}, u32[]{:S(2)}) collective-permute-start(bf16[1024,256]{1,0:T(8,128)(2,1)} %bitcast.3), channel_id=1, source_target_pairs={{0,56},{8,16},{16,8},{24,32},{32,24},{40,48},{48,40},{56,0},{64,12... | collective-permute-start | bytes 1572872 | tf_op jit(solution)/shard_map/ppermute | solution.py:33
  106.8 7.2 %copy-start.1 = (bf16[4,1,4,1,64,512]{5,4,3,2,1,0:T(8,128)(2,1)S(1)}, bf16[4,1,4,1,64,512]{5,4,3,2,1,0:T(8,128)(2,1)}, u32[]{:S(2)}) copy-start(bf16[4,1,4,1,64,512]{5,4,3,2,1,0:T(8,128)(2,1)} %get-tuple-element.28) | copy-start | bytes 3145732
  106.8 16.9 %copy-start.9 = (f32[512,256]{1,0:T(8,128)S(1)}, f32[512,256]{1,0:T(8,128)}, u32[]{:S(2)}) copy-start(f32[512,256]{1,0:T(8,128)} %fusion.16) | copy-start | bytes 1572868
  108.3 34.6 %collective-permute-start.9 = (bf16[1024,256]{1,0:T(8,128)(2,1)}, bf16[1024,256]{1,0:T(8,128)(2,1)}, u32[]{:S(2)}, u32[]{:S(2)}) collective-permute-start(bf16[1024,256]{1,0:T(8,128)(2,1)} %convolution_convert_fusion.2), channel_id=1, source_target_pairs={{0,64},{8,72},{16,80},{24,88},{32,96},{40,104},{48,112},{56,120},{... | collective-permute-start | bytes 1572872 | tf_op jit(solution)/shard_map/ppermute | solution.py:33
  111.8 31.1 %collective-permute-start.10 = (bf16[1024,256]{1,0:T(8,128)(2,1)}, bf16[1024,256]{1,0:T(8,128)(2,1)}, u32[]{:S(2)}, u32[]{:S(2)}) collective-permute-start(bf16[1024,256]{1,0:T(8,128)(2,1)} %convolution_convert_fusion.1), channel_id=1, source_target_pairs={{0,8},{8,0},{16,24},{24,16},{32,40},{40,32},{48,56},{56,48},{64,72... | collective-permute-start | bytes 1572872 | tf_op jit(solution)/shard_map/ppermute | solution.py:33
  115.2 13.2 %copy-start.13 = (s32[256]{0:T(256)S(1)}, s32[256]{0:T(256)}, u32[]{:S(2)}) copy-start(s32[256]{0:T(256)} %param.7) | copy-start | bytes 3076
  115.2 27.8 %copy-start.3 = (bf16[4,1,4,1,64,512]{5,4,3,2,1,0:T(8,128)(2,1)S(1)}, bf16[4,1,4,1,64,512]{5,4,3,2,1,0:T(8,128)(2,1)}, u32[]{:S(2)}) copy-start(bf16[4,1,4,1,64,512]{5,4,3,2,1,0:T(8,128)(2,1)} %copy-done.2) | copy-start | bytes 3145732
  120.3 22.6 %collective-permute-start.11 = (bf16[1024,256]{1,0:T(8,128)(2,1)}, bf16[1024,256]{1,0:T(8,128)(2,1)}, u32[]{:S(2)}, u32[]{:S(2)}) collective-permute-start(bf16[1024,256]{1,0:T(8,128)(2,1)} %convolution_convert_fusion), channel_id=1, source_target_pairs={{0,72},{8,64},{16,88},{24,80},{32,104},{40,96},{48,120},{56,112},{... | collective-permute-start | bytes 1572872 | tf_op jit(solution)/shard_map/ppermute | solution.py:33
  130.5 25.3 %all-to-all-start.1 = ((f32[64,1,640]{2,1,0:T(1,128)}), f32[64,1,640]{2,1,0:T(1,128)S(1)}, u32[]{:S(2)}, u32[]{:S(2)}) async-start(f32[64,1,640]{2,1,0:T(1,128)} %broadcast_in_dim.17), calls=%async_computation.1 | async-start | bytes 327680 | tf_op jit(solution)/shard_map/all_to_all | solution.py:19
  155.8 20.0 %all-to-all-start.4 = ((bf16[16,64,256]{2,1,0:T(8,128)(2,1)}), bf16[16,64,256]{2,1,0:T(8,128)(2,1)S(1)}, u32[]{:S(2)}, u32[]{:S(2)}) async-start(bf16[16,64,256]{2,1,0:T(8,128)(2,1)} %bitcast.21), calls=%async_computation.4 | async-start | bytes 1048576 | tf_op jit(solution)/shard_map/all_to_all | solution.py:107
where the time goes:
time: 179 us; the launch traced here: 178 us
  starting transfers between devices  91.3 us (51%)
  waiting for transfers between devices  50.4 us (28%)
  matrix products  18.1 us (10%)
  local copies, waits for them, and re-layouts  11.7 us (7%)
  other arithmetic  3.08 us (2%)
  between operations  2.99 us (2%)
    all_to_all x4, starting transfers between devices, from_everyone(): lax.all_to_all(jnp.broadcast_to(x[None], (size(axes), *x.shape)), axes, 0...  44.4 us
    ppermute x12, starting transfers between devices, exchanged(): return lax.ppermute(x, VOCAB, pairs)  43.3 us
    all_to_all x4, waiting for transfers between devices, from_everyone(): lax.all_to_all(jnp.broadcast_to(x[None], (size(axes), *x.shape)), axes, 0...  25.1 us
    all_to_all x1, waiting for transfers between devices, shards(): parts = lax.all_to_all(parts, LATTICE, 0, 0, tiled=True)  13.7 us
    dot_general x11, matrix products, product(): lax.dot_general(block, rows, (((0,), (0,)), ((), ())), preferred_element_...  11.8 us
    ppermute x12, waiting for transfers between devices, exchanged(): return lax.ppermute(x, VOCAB, pairs)  11.6 us
    dot_general x4, matrix products, grad_rows(): lax.dot_general(weights[flip], dlogits_b, (((1,), (1,)), ((), ())), prefe...  6.3 us
    broadcast_in_dim x4, local copies, waits for them, and re-layouts, from_everyone(): jnp.broadcast_to(x[None], (size(axes), *x.shape))  3.89 us
  transfers between devices with their start and end apart: 17, of which 7 were waited for; matrix products, arithmetic and copies ran while one was open for 16% of the time, Pallas kernels for 0%

commit v1 on v0

--- a/solution.py
+++ b/solution.py
@@ -7,7 +7,7 @@
 
 Z, Y = ("z_two", "z_one"), ("y_two", "y_one")
 VOCAB = (*Z, *Y)
-LATTICE = ("z_two", "y_two")
+LATTICE, QUAD = ("z_two", "y_two"), ("z_one", "y_one")
 FLIPS = ((1, 0), (0, 1), (1, 1))
 
 
@@ -17,6 +17,12 @@
 
 def from_everyone(x, axes):
     return lax.all_to_all(jnp.broadcast_to(x[None], (size(axes), *x.shape)), axes, 0, 0, tiled=True)
+
+
+def pieces(x):
+    high = lax.reduce_precision(x, 8, 7)
+    middle = lax.reduce_precision(x - high, 8, 7)
+    return high, middle, x - high - middle
 
 
 def neighbour(i, n, shift):
@@ -59,16 +65,16 @@
 
     mine_b = class_rows(hidden_b)
     mine_a = class_rows(hidden_a)
-    scores_b = product(mine_b, weights[0, 0])
-    for flip in FLIPS:
-        for shift in range(2):
-            at = slice(shift * half, (shift + 1) * half)
-            block = exchanged(mine_b[at], flip, shift)
-            scores_b = scores_b + product(block, weights[flip][at])
-    scores_a = product(mine_a, weights[0, 0])
-    for flip in FLIPS:
-        block = exchanged(mine_a, flip, 1)
-        scores_a = scores_a + product(block, weights[flip])
+
+    def scores_of(mine, shift):
+        scores = product(mine, weights[0, 0])
+        for flip in FLIPS:
+            block = exchanged(mine, flip, shift)
+            scores = scores + product(block, weights[flip])
+        return scores
+
+    scores_b = scores_of(mine_b, 0)
+    scores_a = scores_of(mine_a, 1)
     column = offset + lax.broadcasted_iota(jnp.int32, (1, columns), 1)
     column_a = lax.optimization_barrier(column)
 
@@ -84,9 +90,13 @@
     label_own = jnp.sum(jnp.where(column_a == labels_a[:, None], scores_a, 0.0), axis=1)
     largest = jnp.full((128,), jnp.max(jnp.abs(scores_a)))
     line = jnp.concatenate([log_total(scores_a), label_own, largest])
-    lines = from_everyone(line.reshape(1, -1), VOCAB).reshape(-1, line.size)
-    loss_a = joined(lines[:, :tokens]) - jnp.sum(lines[:, tokens : 2 * tokens], axis=0)
-    amax_scale = (448.0 / jnp.max(lines[:, 2 * tokens :])).reshape(1).astype(jnp.float32)
+    quad = from_everyone(line.reshape(1, -1), QUAD).reshape(-1, line.size)
+    log_a = pieces(joined(quad[:, :tokens]))
+    label_a = pieces(jnp.sum(quad[:, tokens : 2 * tokens], axis=0))
+    lane = lax.broadcasted_iota(jnp.int32, (tokens,), 0)
+    high, middle, low = pieces(jnp.max(quad[:, 2 * tokens :]))
+    largest = jnp.where(lane == 0, high, jnp.where(lane == 1, middle, low))
+    riders = jnp.stack([*log_a, *label_a, largest, jnp.zeros_like(largest)]).astype(jnp.bfloat16)
 
     onehot = (column == labels_b[:, None]).astype(jnp.float32)
     dlogits_b = ((jnp.exp(scores_b - log_b[:, None]) - onehot) * loss_cotangent[:, None]).astype(
@@ -100,12 +110,16 @@
             weights[flip], dlogits_b, (((1,), (1,)), ((), ())), preferred_element_type=jnp.float32
         )
 
-    total = grad_rows((0, 0))
+    total = lax.optimization_barrier(grad_rows((0, 0)))
     for flip in FLIPS:
         total = total + exchanged(grad_rows(flip).astype(jnp.bfloat16), flip, 0).astype(jnp.float32)
     parts = total.astype(jnp.bfloat16).reshape(lattice, width, tokens)
+    parts = jnp.concatenate([parts, jnp.broadcast_to(riders[None], (lattice, *riders.shape))], axis=1)
     parts = lax.all_to_all(parts, LATTICE, 0, 0, tiled=True)
-    grad_hidden_b = jnp.sum(parts.astype(jnp.float32), axis=0).astype(jnp.bfloat16).T
+    grad_hidden_b = jnp.sum(parts[:, :width].astype(jnp.float32), axis=0).astype(jnp.bfloat16).T
+    came = parts[:, width:].astype(jnp.float32)
+    loss_a = joined(came[:, :3].sum(axis=1)) - came[:, 3:6].sum(axis=(0, 1))
+    amax_scale = (448.0 / jnp.max(came[:, 6, :3].sum(axis=1))).reshape(1).astype(jnp.float32)
     return (scores_a.astype(jnp.bfloat16), loss_a, amax_scale, grad_hidden_b)
 
 

time: 179 us -> 184 us (1.028)
  the two profiles are of different devices: /device:TPU:2 before, /device:TPU:4 now
where the time goes in v1:
time: 184 us; the launch traced here: 183 us
  starting transfers between devices  54.2 us (29%)
  waiting for transfers between devices  52.9 us (29%)
  blocking collectives  35.5 us (19%)
  matrix products  18 us (10%)
  local copies, waits for them, and re-layouts  8.09 us (4%)
  other arithmetic  7.46 us (4%)
  between operations  6.52 us (4%)
    all_to_all x1, blocking collectives, from_everyone(): lax.all_to_all(jnp.broadcast_to(x[None], (size(axes), *x.shape)), axes, 0...  35.5 us
    ppermute x9, starting transfers between devices, exchanged(): return lax.ppermute(x, VOCAB, pairs)  31.3 us
    all_to_all x1, waiting for transfers between devices, shards(): parts = lax.all_to_all(parts, LATTICE, 0, 0, tiled=True)  20.5 us
    ppermute x9, waiting for transfers between devices, exchanged(): return lax.ppermute(x, VOCAB, pairs)  18.6 us
    all_to_all x3, starting transfers between devices, from_everyone(): lax.all_to_all(jnp.broadcast_to(x[None], (size(axes), *x.shape)), axes, 0...  18.2 us
    all_to_all x3, waiting for transfers between devices, from_everyone(): lax.all_to_all(jnp.broadcast_to(x[None], (size(axes), *x.shape)), axes, 0...  13.8 us
    dot_general x8, matrix products, product(): lax.dot_general(block, rows, (((0,), (0,)), ((), ())), preferred_element_...  13.4 us
    all_to_all x1, starting transfers between devices, shards(): parts = lax.all_to_all(parts, LATTICE, 0, 0, tiled=True)  4.74 us
  transfers between devices with their start and end apart: 13, of which 7 were waited for; matrix products, arithmetic and copies ran while one was open for 12% of the time, Pallas kernels for 0%

profile of v1, /device:TPU:4, one launch (start us, length us, event | category | flops | bytes accessed | tf_op | source)
XLA Modules:
  0.0 182.7 jit_solution(940176874586935300)
XLA Ops:
  0.6 0.8 broadcast_in_dim.28
  1.5 35.5 %all_to_all.25 = bf16[16,64,256]{2,1,0:T(8,128)(2,1)} all-to-all(bf16[16,64,256]{2,1,0:T(8,128)(2,1)S(1)} %broadcast_in_dim.28), channel_id=1, replica_groups=mesh['z_two'=4,'z_one'=2,'y_two'=4,'y_one'=2,'pipe'=8] {'z_two','y_two'}, dimensions={0} | all-to-all | bytes 1048576 | tf_op jit(solution)/shard_map/all_to_all | solution.py:19
  37.0 0.9 broadcast_in_dim.29
  37.9 6.2 %all-to-all-start.1 = ((bf16[16,64,256]{2,1,0:T(8,128)(2,1)}), bf16[16,64,256]{2,1,0:T(8,128)(2,1)}, u32[]{:S(2)}, u32[]{:S(2)}) async-start(bf16[16,64,256]{2,1,0:T(8,128)(2,1)} %broadcast_in_dim.29), calls=%async_computation.1 | async-start | bytes 1048576 | tf_op jit(solution)/shard_map/all_to_all | solution.py:19
  44.1 3.6 %constant_dynamic-slice_fusion.1 = (bf16[4,1,4,1,64,512]{5,4,3,2,1,0:T(8,128)(2,1)S(1)}, bf16[4,1,4,1,64,512]{5,4,3,2,1,0:T(8,128)(2,1)S(1)}, bf16[4,1,4,1,64,51...) fusion(bf16[4,2,4,2,64,512]{5,4,3,2,1,0:T(8,128)(2,1)} %bitcast.76, s32[]{:T(128)S(6)} %select_n.46, ...), kind=kLoop, calls=%fused_computation.59 | loop fusion | bytes 8388624 | tf_op jit(solution)/shard_map/dynamic_slice | solution.py:54
  47.7 6.7 %collective-permute-start.2 = (bf16[1024,256]{1,0:T(8,128)(2,1)}, bf16[1024,256]{1,0:T(8,128)(2,1)}, u32[]{:S(2)}, u32[]{:S(2)}) collective-permute-start(bf16[1024,256]{1,0:T(8,128)(2,1)} %bitcast.3), channel_id=1, source_target_pairs={{0,504},{8,464},{16,456},{24,480},{32,472},{40,496},{48,488},{56,4... | collective-permute-start | bytes 1572872 | tf_op jit(solution)/shard_map/ppermute | solution.py:39
  54.4 1.9 %collective-permute-start = (bf16[1024,256]{1,0:T(8,128)(2,1)}, bf16[1024,256]{1,0:T(8,128)(2,1)}, u32[]{:S(2)}, u32[]{:S(2)}) collective-permute-start(bf16[1024,256]{1,0:T(8,128)(2,1)} %bitcast.3), channel_id=1, source_target_pairs={{0,448},{8,456},{16,464},{24,472},{32,480},{40,488},{48,496},{56,5... | collective-permute-start | bytes 1572872 | tf_op jit(solution)/shard_map/ppermute | solution.py:39
  56.4 3.6 %collective-permute-start.1 = (bf16[1024,256]{1,0:T(8,128)(2,1)}, bf16[1024,256]{1,0:T(8,128)(2,1)}, u32[]{:S(2)}, u32[]{:S(2)}) collective-permute-start(bf16[1024,256]{1,0:T(8,128)(2,1)} %bitcast.3), channel_id=1, source_target_pairs={{0,56},{8,16},{16,8},{24,32},{32,24},{40,48},{48,40},{56,0},{64,12... | collective-permute-start | bytes 1572872 | tf_op jit(solution)/shard_map/ppermute | solution.py:39
  60.0 5.9 %all-to-all-done.1 = bf16[16,64,256]{2,1,0:T(8,128)(2,1)} async-done(((bf16[16,64,256]{2,1,0:T(8,128)(2,1)}), bf16[16,64,256]{2,1,0:T(8,128)(2,1)}, u32[]{:S(2)}, u32[]{:S(2)}) %all-to-all-start.1) | async-done | bytes 524320 | tf_op jit(solution)/shard_map/all_to_all | solution.py:19
  65.8 1.9 %collective-permute-start.5 = (bf16[1024,256]{1,0:T(8,128)(2,1)}, bf16[1024,256]{1,0:T(8,128)(2,1)}, u32[]{:S(2)}, u32[]{:S(2)}) collective-permute-start(bf16[1024,256]{1,0:T(8,128)(2,1)} %bitcast.9), channel_id=1, source_target_pairs={{0,72},{8,64},{16,88},{24,80},{32,104},{40,96},{48,120},{56,112},{... | collective-permute-start | bytes 1572872 | tf_op jit(solution)/shard_map/ppermute | solution.py:39
  67.7 4.6 %collective-permute-start.3 = (bf16[1024,256]{1,0:T(8,128)(2,1)}, bf16[1024,256]{1,0:T(8,128)(2,1)}, u32[]{:S(2)}, u32[]{:S(2)}) collective-permute-start(bf16[1024,256]{1,0:T(8,128)(2,1)} %bitcast.9), channel_id=1, source_target_pairs={{0,64},{8,72},{16,80},{24,88},{32,96},{40,104},{48,112},{56,120},{... | collective-permute-start | bytes 1572872 | tf_op jit(solution)/shard_map/ppermute | solution.py:39
  72.3 1.9 %fusion.15 = f32[512,256]{1,0:T(8,128)S(1)} fusion(bf16[1024,512]{1,0:T(8,128)(2,1)} %bitcast.77, bf16[1024,256]{1,0:T(8,128)(2,1)} %bitcast.3), kind=kOutput, calls=%fused_computation.64 | convolution fusion | flops 268435456 | bytes 2097152 | tf_op jit(solution)/shard_map/dot_general | solution.py:59
  74.2 2.3 %fusion.17 = f32[512,256]{1,0:T(8,128)} fusion(bf16[1024,512]{1,0:T(8,128)(2,1)S(1)} %bitcast.78, bf16[1024,256]{1,0:T(8,128)(2,1)} %bitcast.9), kind=kOutput, calls=%fused_computation.66 | convolution fusion | flops 268435456 | bytes 2097152 | tf_op jit(solution)/shard_map/dot_general | solution.py:59
  76.6 0.0 collective-permute-done.2
  76.6 3.4 %collective-permute-start.4 = (bf16[1024,256]{1,0:T(8,128)(2,1)}, bf16[1024,256]{1,0:T(8,128)(2,1)}, u32[]{:S(2)}, u32[]{:S(2)}) collective-permute-start(bf16[1024,256]{1,0:T(8,128)(2,1)} %bitcast.9), channel_id=1, source_target_pairs={{0,8},{8,0},{16,24},{24,16},{32,40},{40,32},{48,56},{56,48},{64,72... | collective-permute-start | bytes 1572872 | tf_op jit(solution)/shard_map/ppermute | solution.py:39
  79.9 1.5 fusion.16
  81.5 4.1 %collective-permute-done = bf16[1024,256]{1,0:T(8,128)(2,1)} collective-permute-done((bf16[1024,256]{1,0:T(8,128)(2,1)}, bf16[1024,256]{1,0:T(8,128)(2,1)}, u32[]{:S(2)}, u32[]{:S(2)}) %collective-permute-start) | collective-permute-done | bytes 524320 | tf_op jit(solution)/shard_map/ppermute | solution.py:39
  85.5 1.5 convolution_add_fusion.3
  87.1 0.0 collective-permute-done.1
  87.1 0.0 copy-start.5
  87.1 1.5 fusion.13
  88.6 0.7 fusion.5
  89.3 0.7 broadcast_in_dim.32
  90.0 0.6 broadcast_in_dim.33
  90.6 3.3 %all-to-all-start.3 = ((f32[4,1,640]{2,1,0:T(1,128)}), f32[4,1,640]{2,1,0:T(1,128)S(1)}, u32[]{:S(2)}, u32[]{:S(2)}) async-start(f32[4,1,640]{2,1,0:T(1,128)} %broadcast_in_dim.33), calls=%async_computation.3 | async-start | bytes 20480 | tf_op jit(solution)/shard_map/all_to_all | solution.py:19
  93.9 0.0 copy-start.3
  93.9 0.0 collective-permute-done.5
  93.9 1.6 fusion.18
  95.5 0.0 collective-permute-done.3
  95.5 1.5 convolution_add_fusion.1
  97.0 0.0 copy-start.6
  97.0 0.0 copy-start.7
  97.0 0.0 collective-permute-done.4
  97.0 1.5 fusion.14
  98.6 0.1 exponential_reduce_fusion
  98.7 0.0 all-to-all-done.3
  98.7 0.7 broadcast_in_dim.30
  99.4 8.7 %all-to-all-start.2 = ((f32[64,1,256]{2,1,0:T(1,128)}), f32[64,1,256]{2,1,0:T(1,128)S(1)}, u32[]{:S(2)}, u32[]{:S(2)}) async-start(f32[64,1,256]{2,1,0:T(1,128)} %broadcast_in_dim.30), calls=%async_computation.2 | async-start | bytes 131072 | tf_op jit(solution)/shard_map/all_to_all | solution.py:19
  108.1 0.6 slice_reduce_fusion.6
  112.4 7.9 %all-to-all-done.2 = f32[64,1,256]{2,1,0:T(1,128)S(1)} async-done(((f32[64,1,256]{2,1,0:T(1,128)}), f32[64,1,256]{2,1,0:T(1,128)S(1)}, u32[]{:S(2)}, u32[]{:S(2)}) %all-to-all-start.2) | async-done | bytes 65568 | tf_op jit(solution)/shard_map/all_to_all | solution.py:19
  120.3 0.1 reduce_max.73
  120.5 0.0 copy-done.6
  120.5 0.2 fusion.3
  120.7 2.5 %convolution_convert_fusion = bf16[1024,256]{1,0:T(8,128)(2,1)} fusion(bf16[1024,512]{1,0:T(8,128)(2,1)} %bitcast.75, bf16[256,512]{0,1:T(8,128)(2,1)S(1)} %fusion.3), kind=kOutput, calls=%fused_computation | convolution fusion | flops 268697600 | bytes 1835008 | tf_op jit(solution)/shard_map/dot_general | solution.py:109
  123.1 1.3 convolution_convert_fusion.1
  124.4 0.4 convolution_convert_fusion.2
  124.8 2.7 %collective-permute-start.8 = (bf16[1024,256]{1,0:T(8,128)(2,1)}, bf16[1024,256]{1,0:T(8,128)(2,1)S(1)}, u32[]{:S(2)}, u32[]{:S(2)}) collective-permute-start(bf16[1024,256]{1,0:T(8,128)(2,1)} %convolution_convert_fusion), channel_id=1, source_target_pairs={{0,72},{8,64},{16,88},{24,80},{32,104},{40,96},{48,120},{56,112},{... | collective-permute-start | bytes 1572872 | tf_op jit(solution)/shard_map/ppermute | solution.py:39
  127.5 3.2 %collective-permute-start.7 = (bf16[1024,256]{1,0:T(8,128)(2,1)}, bf16[1024,256]{1,0:T(8,128)(2,1)S(1)}, u32[]{:S(2)}, u32[]{:S(2)}) collective-permute-start(bf16[1024,256]{1,0:T(8,128)(2,1)} %convolution_convert_fusion.1), channel_id=1, source_target_pairs={{0,8},{8,0},{16,24},{24,16},{32,40},{40,32},{48,56},{56,48},{64,72... | collective-permute-start | bytes 1572872 | tf_op jit(solution)/shard_map/ppermute | solution.py:39
  130.7 3.3 %collective-permute-start.6 = (bf16[1024,256]{1,0:T(8,128)(2,1)S(1)}, bf16[1024,256]{1,0:T(8,128)(2,1)}, u32[]{:S(2)}, u32[]{:S(2)}) collective-permute-start(bf16[1024,256]{1,0:T(8,128)(2,1)S(1)} %convolution_convert_fusion.2), channel_id=1, source_target_pairs={{0,64},{8,72},{16,80},{24,88},{32,96},{40,104},{48,112},{56,120},{... | collective-permute-start | bytes 1572872 | tf_op jit(solution)/shard_map/ppermute | solution.py:39
  134.0 1.3 fusion.12
  135.4 0.4 fusion.19
  135.9 6.8 %collective-permute-done.8 = bf16[1024,256]{1,0:T(8,128)(2,1)S(1)} collective-permute-done((bf16[1024,256]{1,0:T(8,128)(2,1)}, bf16[1024,256]{1,0:T(8,128)(2,1)S(1)}, u32[]{:S(2)}, u32[]{:S(2)}) %collective-permute-start.8) | collective-permute-done | bytes 524320 | tf_op jit(solution)/shard_map/ppermute | solution.py:39
  142.7 6.8 %collective-permute-done.7 = bf16[1024,256]{1,0:T(8,128)(2,1)S(1)} collective-permute-done((bf16[1024,256]{1,0:T(8,128)(2,1)}, bf16[1024,256]{1,0:T(8,128)(2,1)S(1)}, u32[]{:S(2)}, u32[]{:S(2)}) %collective-permute-start.7) | collective-permute-done | bytes 524320 | tf_op jit(solution)/shard_map/ppermute | solution.py:39
  149.5 0.9 collective-permute-done.6
  150.4 1.3 add_convert_fusion
  151.7 0.8 pad_maximum_fusion
  152.6 4.7 %all-to-all-start.4 = ((bf16[16,72,256]{2,1,0:T(8,128)(2,1)}), bf16[16,72,256]{2,1,0:T(8,128)(2,1)S(1)}, u32[]{:S(2)}, u32[]{:S(2)}) async-start(bf16[16,72,256]{2,1,0:T(8,128)(2,1)} %pad_maximum_fusion), calls=%async_computation.4 | async-start | bytes 1179648 | tf_op jit(solution)/shard_map/all_to_all | solution.py:118
  157.3 0.8 copy.13
  158.2 20.5 %all-to-all-done.4 = bf16[16,72,256]{2,1,0:T(8,128)(2,1)S(1)} async-done(((bf16[16,72,256]{2,1,0:T(8,128)(2,1)}), bf16[16,72,256]{2,1,0:T(8,128)(2,1)S(1)}, u32[]{:S(2)}, u32[]{:S(2)}) %all-to-all-start.4) | async-done | bytes 589856 | tf_op jit(solution)/shard_map/all_to_all | solution.py:118
  178.7 0.1 slice_reduce_fusion.2
  178.7 0.2 slice_reduce_fusion.3
  179.0 0.6 reduce_max.79
  179.6 0.6 add_subtract_fusion
  180.8 0.7 slice_reduce_fusion
  (29 shorter events, 0.3 us)
Async XLA Ops:
  0.6 36.4 %copy-start.4 = (bf16[256,64]{0,1:T(8,128)(2,1)S(1)}, bf16[256,64]{0,1:T(8,128)(2,1)}, u32[]{:S(2)}) copy-start(bf16[256,64]{0,1:T(8,128)(2,1)} %param.8) | copy-start | bytes 98308
  37.9 28.0 %all-to-all-start.1 = ((bf16[16,64,256]{2,1,0:T(8,128)(2,1)}), bf16[16,64,256]{2,1,0:T(8,128)(2,1)}, u32[]{:S(2)}, u32[]{:S(2)}) async-start(bf16[16,64,256]{2,1,0:T(8,128)(2,1)} %broadcast_in_dim.29), calls=%async_computation.1 | async-start | bytes 1048576 | tf_op jit(solution)/shard_map/all_to_all | solution.py:19
  47.7 46.2 %copy-start = (bf16[4,1,4,1,64,512]{5,4,3,2,1,0:T(8,128)(2,1)}, bf16[4,1,4,1,64,512]{5,4,3,2,1,0:T(8,128)(2,1)S(1)}, u32[]{:S(2)}) copy-start(bf16[4,1,4,1,64,512]{5,4,3,2,1,0:T(8,128)(2,1)S(1)} %get-tuple-element.24) | copy-start | bytes 3145732
  47.7 28.9 %collective-permute-start.2 = (bf16[1024,256]{1,0:T(8,128)(2,1)}, bf16[1024,256]{1,0:T(8,128)(2,1)}, u32[]{:S(2)}, u32[]{:S(2)}) collective-permute-start(bf16[1024,256]{1,0:T(8,128)(2,1)} %bitcast.3), channel_id=1, source_target_pairs={{0,504},{8,464},{16,456},{24,480},{32,472},{40,496},{48,488},{56,4... | collective-permute-start | bytes 1572872 | tf_op jit(solution)/shard_map/ppermute | solution.py:39
  54.4 31.1 %collective-permute-start = (bf16[1024,256]{1,0:T(8,128)(2,1)}, bf16[1024,256]{1,0:T(8,128)(2,1)}, u32[]{:S(2)}, u32[]{:S(2)}) collective-permute-start(bf16[1024,256]{1,0:T(8,128)(2,1)} %bitcast.3), channel_id=1, source_target_pairs={{0,448},{8,456},{16,464},{24,472},{32,480},{40,488},{48,496},{56,5... | collective-permute-start | bytes 1572872 | tf_op jit(solution)/shard_map/ppermute | solution.py:39
  56.4 30.7 %collective-permute-start.1 = (bf16[1024,256]{1,0:T(8,128)(2,1)}, bf16[1024,256]{1,0:T(8,128)(2,1)}, u32[]{:S(2)}, u32[]{:S(2)}) collective-permute-start(bf16[1024,256]{1,0:T(8,128)(2,1)} %bitcast.3), channel_id=1, source_target_pairs={{0,56},{8,16},{16,8},{24,32},{32,24},{40,48},{48,40},{56,0},{64,12... | collective-permute-start | bytes 1572872 | tf_op jit(solution)/shard_map/ppermute | solution.py:39
  65.8 28.1 %collective-permute-start.5 = (bf16[1024,256]{1,0:T(8,128)(2,1)}, bf16[1024,256]{1,0:T(8,128)(2,1)}, u32[]{:S(2)}, u32[]{:S(2)}) collective-permute-start(bf16[1024,256]{1,0:T(8,128)(2,1)} %bitcast.9), channel_id=1, source_target_pairs={{0,72},{8,64},{16,88},{24,80},{32,104},{40,96},{48,120},{56,112},{... | collective-permute-start | bytes 1572872 | tf_op jit(solution)/shard_map/ppermute | solution.py:39
  67.7 27.7 %collective-permute-start.3 = (bf16[1024,256]{1,0:T(8,128)(2,1)}, bf16[1024,256]{1,0:T(8,128)(2,1)}, u32[]{:S(2)}, u32[]{:S(2)}) collective-permute-start(bf16[1024,256]{1,0:T(8,128)(2,1)} %bitcast.9), channel_id=1, source_target_pairs={{0,64},{8,72},{16,80},{24,88},{32,96},{40,104},{48,112},{56,120},{... | collective-permute-start | bytes 1572872 | tf_op jit(solution)/shard_map/ppermute | solution.py:39
  72.3 1.9 %copy-start.1 = (bf16[4,1,4,1,64,512]{5,4,3,2,1,0:T(8,128)(2,1)S(1)}, bf16[4,1,4,1,64,512]{5,4,3,2,1,0:T(8,128)(2,1)}, u32[]{:S(2)}) copy-start(bf16[4,1,4,1,64,512]{5,4,3,2,1,0:T(8,128)(2,1)} %get-tuple-element.26) | copy-start | bytes 3145732
  76.6 20.5 %collective-permute-start.4 = (bf16[1024,256]{1,0:T(8,128)(2,1)}, bf16[1024,256]{1,0:T(8,128)(2,1)}, u32[]{:S(2)}, u32[]{:S(2)}) collective-permute-start(bf16[1024,256]{1,0:T(8,128)(2,1)} %bitcast.9), channel_id=1, source_target_pairs={{0,8},{8,0},{16,24},{24,16},{32,40},{40,32},{48,56},{56,48},{64,72... | collective-permute-start | bytes 1572872 | tf_op jit(solution)/shard_map/ppermute | solution.py:39
  87.1 1.6 copy-start.5
  90.6 8.1 %all-to-all-start.3 = ((f32[4,1,640]{2,1,0:T(1,128)}), f32[4,1,640]{2,1,0:T(1,128)S(1)}, u32[]{:S(2)}, u32[]{:S(2)}) async-start(f32[4,1,640]{2,1,0:T(1,128)} %broadcast_in_dim.33), calls=%async_computation.3 | async-start | bytes 20480 | tf_op jit(solution)/shard_map/all_to_all | solution.py:19
  93.9 1.6 copy-start.3
  97.0 23.5 %copy-start.6 = (f32[256]{0:T(256)S(1)}, f32[256]{0:T(256)}, u32[]{:S(2)}) copy-start(f32[256]{0:T(256)} %param.10) | copy-start | bytes 3076
  97.0 23.5 %copy-start.7 = (s32[256]{0:T(256)S(1)}, s32[256]{0:T(256)}, u32[]{:S(2)}) copy-start(s32[256]{0:T(256)} %param.9) | copy-start | bytes 3076
  99.4 20.9 %all-to-all-start.2 = ((f32[64,1,256]{2,1,0:T(1,128)}), f32[64,1,256]{2,1,0:T(1,128)S(1)}, u32[]{:S(2)}, u32[]{:S(2)}) async-start(f32[64,1,256]{2,1,0:T(1,128)} %broadcast_in_dim.30), calls=%async_computation.2 | async-start | bytes 131072 | tf_op jit(solution)/shard_map/all_to_all | solution.py:19
  124.4 11.0 %copy-start.2 = (bf16[4,1,4,1,64,512]{5,4,3,2,1,0:T(8,128)(2,1)S(1)}, bf16[4,1,4,1,64,512]{5,4,3,2,1,0:T(8,128)(2,1)}, u32[]{:S(2)}) copy-start(bf16[4,1,4,1,64,512]{5,4,3,2,1,0:T(8,128)(2,1)} %get-tuple-element.26) | copy-start | bytes 3145732
  124.8 17.8 %collective-permute-start.8 = (bf16[1024,256]{1,0:T(8,128)(2,1)}, bf16[1024,256]{1,0:T(8,128)(2,1)S(1)}, u32[]{:S(2)}, u32[]{:S(2)}) collective-permute-start(bf16[1024,256]{1,0:T(8,128)(2,1)} %convolution_convert_fusion), channel_id=1, source_target_pairs={{0,72},{8,64},{16,88},{24,80},{32,104},{40,96},{48,120},{56,112},{... | collective-permute-start | bytes 1572872 | tf_op jit(solution)/shard_map/ppermute | solution.py:39
  127.5 22.0 %collective-permute-start.7 = (bf16[1024,256]{1,0:T(8,128)(2,1)}, bf16[1024,256]{1,0:T(8,128)(2,1)S(1)}, u32[]{:S(2)}, u32[]{:S(2)}) collective-permute-start(bf16[1024,256]{1,0:T(8,128)(2,1)} %convolution_convert_fusion.1), channel_id=1, source_target_pairs={{0,8},{8,0},{16,24},{24,16},{32,40},{40,32},{48,56},{56,48},{64,72... | collective-permute-start | bytes 1572872 | tf_op jit(solution)/shard_map/ppermute | solution.py:39
  130.7 19.7 %collective-permute-start.6 = (bf16[1024,256]{1,0:T(8,128)(2,1)S(1)}, bf16[1024,256]{1,0:T(8,128)(2,1)}, u32[]{:S(2)}, u32[]{:S(2)}) collective-permute-start(bf16[1024,256]{1,0:T(8,128)(2,1)S(1)} %convolution_convert_fusion.2), channel_id=1, source_target_pairs={{0,64},{8,72},{16,80},{24,88},{32,96},{40,104},{48,112},{56,120},{... | collective-permute-start | bytes 1572872 | tf_op jit(solution)/shard_map/ppermute | solution.py:39
  152.6 26.1 %all-to-all-start.4 = ((bf16[16,72,256]{2,1,0:T(8,128)(2,1)}), bf16[16,72,256]{2,1,0:T(8,128)(2,1)S(1)}, u32[]{:S(2)}, u32[]{:S(2)}) async-start(bf16[16,72,256]{2,1,0:T(8,128)(2,1)} %pad_maximum_fusion), calls=%async_computation.4 | async-start | bytes 1179648 | tf_op jit(solution)/shard_map/all_to_all | solution.py:118
